TPU v7x, 32 devices: a whole 2x2x4 slice. The times are simulated.
32 devices in a mesh: gx: 4 (over x, core), gy: 4 (over z), gz: 2 (over y).
Axes of the slice: x: 2, y: 2, z: 4, core: 2. Of those that a mesh axis runs over, the one named last changes fastest.
Arguments:
- field: float32 [64, 1024, 256], P('gx', 'gy', 'gz'), may hold values from -6 to 6
- source: float32 [64, 1024, 256], P('gx', 'gy', 'gz'), may hold values from -6 to 6
Outputs:
- smoothed: float32 [64, 1024, 256], P('gx', 'gy', 'gz')
All inputs are finite; a program needn't handle non-finite values.
Results may differ from a plain program's by a relative error of at most 0.00002.
Values sent between devices are 32-bit elements; how exact they have to be, the bound alone decides.
A program may use at most 64 MiB of HBM per device.

v0:
```python
import jax
import jax.numpy as jnp
from jax import lax
from jax.sharding import PartitionSpec as P

SWEEPS = 3


def extended_2(block, sides, width):
    for axis, dim in sides:
        count = lax.axis_size(axis)
        forward = [(i, i + 1) for i in range(count - 1)]
        forward.append((count - 1, 0))
        backward = [(target, source) for source, target in forward]
        low = lax.ppermute(
            lax.slice_in_dim(block, block.shape[dim] - width, None, axis=dim), axis, forward
        )
        high = lax.ppermute(lax.slice_in_dim(block, 0, width, axis=dim), axis, backward)
        block = jnp.concatenate([low, block, high], axis=dim)
    return block


def wall_mask(length, width):
    position = jnp.arange(length, dtype=jnp.int32)
    index = lax.axis_index("gx")
    last = lax.axis_size("gx") - 1
    outside = (position < width) & (index == 0) | (position >= length - width) & (index == last)
    return jnp.where(outside, 0.0, 1.0).astype(jnp.float32)[:, None, None]


def parity_of(shape, offset):
    total = (
        lax.broadcasted_iota(jnp.int32, shape, 0)
        + lax.broadcasted_iota(jnp.int32, shape, 1)
        + lax.broadcasted_iota(jnp.int32, shape, 2)
    )
    return (total + offset) % 2


def neighbours(padded):
    beside = padded[2:, 1:-1, 1:-1] + padded[:-2, 1:-1, 1:-1]
    beside = beside + padded[1:-1, 2:, 1:-1] + padded[1:-1, :-2, 1:-1]
    beside = beside + padded[1:-1, 1:-1, 2:] + padded[1:-1, 1:-1, :-2]
    return beside


def on_device(field, source):
    values = field
    parity = parity_of(values.shape, 0)
    wide_walls = wall_mask(values.shape[0] + 4, 2)
    walls = wall_mask(values.shape[0] + 2, 1)
    source_ext = extended_2(source, (("gx", 0), ("gy", 1), ("gz", 2)), 1)
    parity_ext = parity_of(source_ext.shape, 1)
    for sweep in range(SWEEPS):
        padded = extended_2(values, (("gx", 0), ("gy", 1), ("gz", 2)), 2) * wide_walls
        extended = padded[1:-1, 1:-1, 1:-1]
        extended = (
            jnp.where(parity_ext == 0, (source_ext + neighbours(padded)) / 6.0, extended) * walls
        )
        values = jnp.where(
            parity == 1, (source + neighbours(extended)) / 6.0, extended[1:-1, 1:-1, 1:-1]
        )
    return values


def solution(mesh):
    in_specs = (P("gx", "gy", "gz"), P("gx", "gy", "gz"))
    out_specs = P("gx", "gy", "gz")
    return jax.shard_map(
        on_device, mesh=mesh, in_specs=in_specs, out_specs=out_specs, check_vma=False
    )
```

profile of v0, /device:TPU:0, one launch (start us, length us, event | category | flops | bytes accessed | tf_op | source)
XLA Modules:
  0.0 237.1 jit_solution(11606779689628017366)
XLA Ops:
  25.0 3.7 %copy.16 = f32[18,258,1]{1,0,2:T(8,128)S(1)} copy(f32[18,258,1]{2,0,1:T(8,128)} %get-tuple-element.11) | data formatting | bytes 37152 | tf_op jit(solution)/shard_map/slice | solution.py:16
  28.7 3.7 %copy.17 = f32[18,258,1]{1,0,2:T(8,128)S(1)} copy(f32[18,258,1]{2,0,1:T(8,128)} %get-tuple-element.12) | data formatting | bytes 37152 | tf_op jit(solution)/shard_map/slice | solution.py:18
  36.6 3.7 %fusion.21 = (f32[20,260,2]{2,0,1:T(8,128)}, f32[20,260,2]{2,0,1:T(8,128)}) fusion(f32[20,260,128]{2,0,1:T(8,128)S(1)} %pad_maximum_fusion.1), kind=kLoop, calls=%fused_computation.85 | loop fusion | bytes 166400 | tf_op jit(solution)/shard_map/slice | solution.py:16
  40.3 3.7 %copy.23 = f32[20,260,2]{1,0,2:T(8,128)S(1)} copy(f32[20,260,2]{2,0,1:T(8,128)} %get-tuple-element.9) | data formatting | bytes 83200 | tf_op jit(solution)/shard_map/slice | solution.py:16
  44.1 3.8 %copy.24 = f32[20,260,2]{1,0,2:T(8,128)S(1)} copy(f32[20,260,2]{2,0,1:T(8,128)} %get-tuple-element.10) | data formatting | bytes 83200 | tf_op jit(solution)/shard_map/slice | solution.py:18
  64.1 9.0 %maximum_multiply_fusion = f32[20,260,132]{2,0,1:T(8,128)S(1)} fusion(f32[20,260,2]{2,0,1:T(8,128)} %copy.26, f32[20,2,128]{2,0,1:T(8,128)S(1)} %collective-permute-done.9, f32[2,256,128]{2,0,1:T(2,128)S(1)} %copy.22, f32[16,256,128]{2,0,1:T(8,128)} %copy-done.2, f32[2,256,128]{2,0,1:T(2,128)S(1)} %copy.20, f32[20,2,128]{2,0,1:T(8,128)S(1)} %collective-permute-done.8, ...), kind=kLoop, calls=%fused_computation.3 | loop fusion | flops 4804800 | bytes 5491280 | tf_op jit(solution)/shard_map/mul | solution.py:55
  73.1 18.5 %fusion.8 = f32[18,258,130]{2,0,1:T(8,128)S(1)} fusion(f32[20,260,132]{2,0,1:T(8,128)S(1)} %maximum_multiply_fusion, f32[18]{0:T(128)S(1)} %or_select_fusion, f32[18,258,1]{2,0,1:T(8,128)} %copy.19, f32[18,1,128]{2,0,1:T(8,128)S(1)} %collective-permute-done.3, f32[1,256,128]{2,0,1:T(1,128)S(1)} %bitcast.9, f32[16,256,128]{2,0,1:T(8,128)S(1)} %copy.45, ...), kind=kLoop, calls=%fused_computation.27 | loop fusion | flops 18111600 | bytes 21733992 | tf_op jit(solution)/shard_map/mul | solution.py:58
  91.6 5.6 %slice_select_fusion.5 = f32[16,256,128]{2,0,1:T(8,128)S(1)} fusion(f32[18,258,130]{2,0,1:T(8,128)S(1)} %fusion.8, f32[16,256,128]{2,1,0:T(8,128)} %param.3), kind=kLoop, calls=%fused_computation.61 | loop fusion | flops 11534336 | bytes 18874368 | tf_op jit(solution)/shard_map/jit(_where)/select_n | solution.py:60
  98.1 5.0 %collective-permute-done.13 = f32[2,256,128]{2,1,0:T(8,128)S(1)} collective-permute-done((f32[2,256,128]{2,1,0:T(8,128)S(1)}, f32[2,256,128]{2,1,0:T(8,128)S(1)}, u32[]{:S(2)}, u32[]{:S(2)}) %collective-permute-start.13) | collective-permute-done | bytes 262176 | tf_op jit(solution)/shard_map/ppermute | solution.py:18
  106.4 3.8 %collective-permute-start.15 = (f32[20,2,128]{2,0,1:T(8,128)S(1)}, f32[20,2,128]{2,0,1:T(8,128)S(1)}, u32[]{:S(2)}, u32[]{:S(2)}) collective-permute-start(f32[20,2,128]{2,0,1:T(8,128)S(1)} %get-tuple-element.16), channel_id=1, source_target_pairs={{2,0},{4,2},{6,4},{0,6},{3,1},{5,3},{7,5},{1,7},{10,8},{12,10},{14... | collective-permute-start | bytes 61448 | tf_op jit(solution)/shard_map/ppermute | solution.py:18
  112.5 3.7 %fusion.20 = (f32[20,260,2]{2,0,1:T(8,128)}, f32[20,260,2]{2,0,1:T(8,128)}) fusion(f32[20,260,128]{2,0,1:T(8,128)S(1)} %pad_maximum_fusion.2), kind=kLoop, calls=%fused_computation.84 | loop fusion | bytes 166400 | tf_op jit(solution)/shard_map/slice | solution.py:16
  116.2 4.1 %copy.32 = f32[20,260,2]{1,0,2:T(8,128)S(1)} copy(f32[20,260,2]{2,0,1:T(8,128)} %get-tuple-element.7) | data formatting | bytes 83200 | tf_op jit(solution)/shard_map/slice | solution.py:16
  122.2 3.7 %copy.33 = f32[20,260,2]{1,0,2:T(8,128)S(1)} copy(f32[20,260,2]{2,0,1:T(8,128)} %get-tuple-element.8) | data formatting | bytes 83200 | tf_op jit(solution)/shard_map/slice | solution.py:18
  133.9 8.8 %maximum_multiply_fusion.1 = f32[20,260,132]{2,0,1:T(8,128)S(1)} fusion(f32[20,260,2]{2,0,1:T(8,128)} %copy.35, f32[20,2,128]{2,0,1:T(8,128)S(1)} %collective-permute-done.15, f32[2,256,128]{2,0,1:T(2,128)S(1)} %copy.31, f32[16,256,128]{2,0,1:T(8,128)} %copy-done.1, f32[2,256,128]{2,0,1:T(2,128)S(1)} %copy.30, f32[20,2,128]{2,0,1:T(8,128)S(1)} %collective-permute-done.14, ...), kind=kLoop, calls=%fused_computation.4 | loop fusion | flops 4804800 | bytes 5491280 | tf_op jit(solution)/shard_map/mul | solution.py:55
  142.7 18.5 %fusion.5 = f32[18,258,130]{2,0,1:T(8,128)S(1)} fusion(f32[20,260,132]{2,0,1:T(8,128)S(1)} %maximum_multiply_fusion.1, f32[18]{0:T(128)S(1)} %or_select_fusion, f32[18,258,1]{2,0,1:T(8,128)} %copy.19, f32[18,1,128]{2,0,1:T(8,128)S(1)} %collective-permute-done.3, f32[1,256,128]{2,0,1:T(1,128)S(1)} %bitcast.10, f32[16,256,128]{2,0,1:T(8,128)S(1)} %copy.45, ...), kind=kLoop, calls=%fused_computation.18 | loop fusion | flops 18111600 | bytes 21733992 | tf_op jit(solution)/shard_map/mul | solution.py:58
  161.2 5.6 %slice_select_fusion.4 = f32[16,256,128]{2,0,1:T(8,128)S(1)} fusion(f32[18,258,130]{2,0,1:T(8,128)S(1)} %fusion.5, f32[16,256,128]{2,1,0:T(8,128)} %param.3), kind=kLoop, calls=%fused_computation.53 | loop fusion | flops 11534336 | bytes 18874368 | tf_op jit(solution)/shard_map/jit(_where)/select_n | solution.py:60
  167.7 6.1 %collective-permute-done.19 = f32[2,256,128]{2,1,0:T(8,128)S(1)} collective-permute-done((f32[2,256,128]{2,1,0:T(8,128)S(1)}, f32[2,256,128]{2,1,0:T(8,128)S(1)}, u32[]{:S(2)}, u32[]{:S(2)}) %collective-permute-start.19) | collective-permute-done | bytes 262176 | tf_op jit(solution)/shard_map/ppermute | solution.py:18
  175.1 3.9 %collective-permute-start.21 = (f32[20,2,128]{2,0,1:T(8,128)S(1)}, f32[20,2,128]{2,0,1:T(8,128)S(1)}, u32[]{:S(2)}, u32[]{:S(2)}) collective-permute-start(f32[20,2,128]{2,0,1:T(8,128)S(1)} %get-tuple-element.14), channel_id=1, source_target_pairs={{2,0},{4,2},{6,4},{0,6},{3,1},{5,3},{7,5},{1,7},{10,8},{12,10},{14... | collective-permute-start | bytes 61448 | tf_op jit(solution)/shard_map/ppermute | solution.py:18
  181.4 3.7 %fusion.19 = (f32[20,260,2]{2,0,1:T(8,128)}, f32[20,260,2]{2,0,1:T(8,128)}) fusion(f32[20,260,128]{2,0,1:T(8,128)S(1)} %pad_maximum_fusion.3), kind=kLoop, calls=%fused_computation.83 | loop fusion | bytes 166400 | tf_op jit(solution)/shard_map/slice | solution.py:16
  185.1 3.9 %copy.41 = f32[20,260,2]{1,0,2:T(8,128)S(1)} copy(f32[20,260,2]{2,0,1:T(8,128)} %get-tuple-element.5) | data formatting | bytes 83200 | tf_op jit(solution)/shard_map/slice | solution.py:16
  190.3 3.7 %copy.42 = f32[20,260,2]{1,0,2:T(8,128)S(1)} copy(f32[20,260,2]{2,0,1:T(8,128)} %get-tuple-element.6) | data formatting | bytes 83200 | tf_op jit(solution)/shard_map/slice | solution.py:18
  202.0 8.8 %maximum_multiply_fusion.2 = f32[20,260,132]{2,0,1:T(8,128)S(1)} fusion(f32[20,260,2]{2,0,1:T(8,128)} %copy.44, f32[20,2,128]{2,0,1:T(8,128)S(1)} %collective-permute-done.21, f32[2,256,128]{2,0,1:T(2,128)S(1)} %copy.40, f32[16,256,128]{2,0,1:T(8,128)} %copy-done, f32[2,256,128]{2,0,1:T(2,128)S(1)} %copy.39, f32[20,2,128]{2,0,1:T(8,128)S(1)} %collective-permute-done.20, ...), kind=kLoop, calls=%fused_computation.5 | loop fusion | flops 4804800 | bytes 5491280 | tf_op jit(solution)/shard_map/mul | solution.py:55
  210.8 18.5 %fusion.2 = f32[18,258,130]{2,0,1:T(8,128)S(1)} fusion(f32[20,260,132]{2,0,1:T(8,128)S(1)} %maximum_multiply_fusion.2, f32[18]{0:T(128)S(1)} %or_select_fusion, f32[18,258,1]{2,0,1:T(8,128)} %copy.19, f32[18,1,128]{2,0,1:T(8,128)S(1)} %collective-permute-done.3, f32[1,256,128]{2,0,1:T(1,128)S(1)} %bitcast.11, f32[16,256,128]{2,0,1:T(8,128)S(1)} %copy.45, ...), kind=kLoop, calls=%fused_computation.9 | loop fusion | flops 18111600 | bytes 21733992 | tf_op jit(solution)/shard_map/mul | solution.py:58
  229.3 5.6 %slice_select_fusion.3 = f32[16,256,128]{2,0,1:T(8,128)S(1)} fusion(f32[18,258,130]{2,0,1:T(8,128)S(1)} %fusion.2, f32[16,256,128]{2,1,0:T(8,128)} %param.3), kind=kLoop, calls=%fused_computation.45 | loop fusion | flops 11534336 | bytes 18874368 | tf_op jit(solution)/shard_map/jit(_where)/select_n | solution.py:60
  (88 shorter events, 77.2 us)
Async XLA Ops:
  1.6 8.1 %collective-permute-start = (f32[1,256,128]{2,1,0:T(8,128)}, f32[1,256,128]{2,1,0:T(8,128)S(1)}, u32[]{:S(2)}, u32[]{:S(2)}) collective-permute-start(f32[1,256,128]{2,1,0:T(8,128)} %get-tuple-element.25), channel_id=1, source_target_pairs={{0,8},{8,16},{16,24},{24,0},{1,9},{9,17},{17,25},{25,1},{2,10},{10... | collective-permute-start | bytes 393224 | tf_op jit(solution)/shard_map/ppermute | solution.py:15
  2.1 7.6 %collective-permute-start.1 = (f32[1,256,128]{2,1,0:T(8,128)S(1)}, f32[1,256,128]{2,1,0:T(8,128)S(1)}, u32[]{:S(2)}, u32[]{:S(2)}) collective-permute-start(f32[1,256,128]{2,1,0:T(8,128)S(1)} %get-tuple-element.26), channel_id=1, source_target_pairs={{8,0},{16,8},{24,16},{0,24},{9,1},{17,9},{25,17},{1,25},{10,2},{18... | collective-permute-start | bytes 393224 | tf_op jit(solution)/shard_map/ppermute | solution.py:18
  5.1 11.4 %collective-permute-start.6 = (f32[2,256,128]{2,1,0:T(8,128)S(1)}, f32[2,256,128]{2,1,0:T(8,128)S(1)}, u32[]{:S(2)}, u32[]{:S(2)}) collective-permute-start(f32[2,256,128]{2,1,0:T(8,128)S(1)} %get-tuple-element.27), channel_id=1, source_target_pairs={{0,8},{8,16},{16,24},{24,0},{1,9},{9,17},{17,25},{25,1},{2,10},{10... | collective-permute-start | bytes 786440 | tf_op jit(solution)/shard_map/ppermute | solution.py:15
  5.8 10.9 %collective-permute-start.7 = (f32[2,256,128]{2,1,0:T(8,128)S(1)}, f32[2,256,128]{2,1,0:T(8,128)S(1)}, u32[]{:S(2)}, u32[]{:S(2)}) collective-permute-start(f32[2,256,128]{2,1,0:T(8,128)S(1)} %get-tuple-element.28), channel_id=1, source_target_pairs={{8,0},{16,8},{24,16},{0,24},{9,1},{17,9},{25,17},{1,25},{10,2},{18... | collective-permute-start | bytes 786440 | tf_op jit(solution)/shard_map/ppermute | solution.py:18
  9.8 6.2 %collective-permute-start.2 = (f32[18,1,128]{2,0,1:T(8,128)S(1)}, f32[18,1,128]{2,0,1:T(8,128)S(1)}, u32[]{:S(2)}, u32[]{:S(2)}) collective-permute-start(f32[18,1,128]{2,0,1:T(8,128)S(1)} %get-tuple-element.19), channel_id=1, source_target_pairs={{0,2},{2,4},{4,6},{6,0},{1,3},{3,5},{5,7},{7,1},{8,10},{10,12},{12... | collective-permute-start | bytes 27656 | tf_op jit(solution)/shard_map/ppermute | solution.py:15
  12.2 3.8 %collective-permute-start.3 = (f32[18,1,128]{2,0,1:T(8,128)S(1)}, f32[18,1,128]{2,0,1:T(8,128)S(1)}, u32[]{:S(2)}, u32[]{:S(2)}) collective-permute-start(f32[18,1,128]{2,0,1:T(8,128)S(1)} %get-tuple-element.20), channel_id=1, source_target_pairs={{2,0},{4,2},{6,4},{0,6},{3,1},{5,3},{7,5},{1,7},{10,8},{12,10},{14... | collective-permute-start | bytes 27656 | tf_op jit(solution)/shard_map/ppermute | solution.py:18
  17.0 17.6 %collective-permute-start.8 = (f32[20,2,128]{2,0,1:T(8,128)S(1)}, f32[20,2,128]{2,0,1:T(8,128)S(1)}, u32[]{:S(2)}, u32[]{:S(2)}) collective-permute-start(f32[20,2,128]{2,0,1:T(8,128)S(1)} %get-tuple-element.17), channel_id=1, source_target_pairs={{0,2},{2,4},{4,6},{6,0},{1,3},{3,5},{5,7},{7,1},{8,10},{10,12},{12... | collective-permute-start | bytes 61448 | tf_op jit(solution)/shard_map/ppermute | solution.py:15
  18.5 16.1 %collective-permute-start.9 = (f32[20,2,128]{2,0,1:T(8,128)S(1)}, f32[20,2,128]{2,0,1:T(8,128)S(1)}, u32[]{:S(2)}, u32[]{:S(2)}) collective-permute-start(f32[20,2,128]{2,0,1:T(8,128)S(1)} %get-tuple-element.18), channel_id=1, source_target_pairs={{2,0},{4,2},{6,4},{0,6},{3,1},{5,3},{7,5},{1,7},{10,8},{12,10},{14... | collective-permute-start | bytes 61448 | tf_op jit(solution)/shard_map/ppermute | solution.py:18
  32.5 21.0 %collective-permute-start.5 = (f32[18,258,1]{1,0,2:T(8,128)S(1)}, f32[18,258,1]{1,0,2:T(8,128)S(1)}, u32[]{:S(2)}, u32[]{:S(2)}) collective-permute-start(f32[18,258,1]{1,0,2:T(8,128)S(1)} %copy.17), channel_id=1, source_target_pairs={{1,0},{0,1},{3,2},{2,3},{5,4},{4,5},{7,6},{6,7},{9,8},{8,9},{11,10... | collective-permute-start | bytes 55736 | tf_op jit(solution)/shard_map/ppermute | solution.py:18
  34.2 15.7 %collective-permute-start.4 = (f32[18,258,1]{1,0,2:T(8,128)S(1)}, f32[18,258,1]{1,0,2:T(8,128)S(1)}, u32[]{:S(2)}, u32[]{:S(2)}) collective-permute-start(f32[18,258,1]{1,0,2:T(8,128)S(1)} %copy.16), channel_id=1, source_target_pairs={{0,1},{1,0},{2,3},{3,2},{4,5},{5,4},{6,7},{7,6},{8,9},{9,8},{10,11... | collective-permute-start | bytes 55736 | tf_op jit(solution)/shard_map/ppermute | solution.py:15
  47.9 12.7 %collective-permute-start.11 = (f32[20,260,2]{1,0,2:T(8,128)S(1)}, f32[20,260,2]{1,0,2:T(8,128)S(1)}, u32[]{:S(2)}, u32[]{:S(2)}) collective-permute-start(f32[20,260,2]{1,0,2:T(8,128)S(1)} %copy.24), channel_id=1, source_target_pairs={{1,0},{0,1},{3,2},{2,3},{5,4},{4,5},{7,6},{6,7},{9,8},{8,9},{11,10... | collective-permute-start | bytes 124808 | tf_op jit(solution)/shard_map/ppermute | solution.py:18
  49.6 7.4 %collective-permute-start.10 = (f32[20,260,2]{1,0,2:T(8,128)S(1)}, f32[20,260,2]{1,0,2:T(8,128)S(1)}, u32[]{:S(2)}, u32[]{:S(2)}) collective-permute-start(f32[20,260,2]{1,0,2:T(8,128)S(1)} %copy.23), channel_id=1, source_target_pairs={{0,1},{1,0},{2,3},{3,2},{4,5},{5,4},{6,7},{7,6},{8,9},{9,8},{10,11... | collective-permute-start | bytes 124808 | tf_op jit(solution)/shard_map/ppermute | solution.py:15
  97.5 5.6 %collective-permute-start.13 = (f32[2,256,128]{2,1,0:T(8,128)S(1)}, f32[2,256,128]{2,1,0:T(8,128)S(1)}, u32[]{:S(2)}, u32[]{:S(2)}) collective-permute-start(f32[2,256,128]{2,1,0:T(8,128)S(1)} %copy.29), channel_id=1, source_target_pairs={{8,0},{16,8},{24,16},{0,24},{9,1},{17,9},{25,17},{1,25},{10,2},{18... | collective-permute-start | bytes 786440 | tf_op jit(solution)/shard_map/ppermute | solution.py:18
  97.6 8.5 %collective-permute-start.12 = (f32[2,256,128]{2,1,0:T(8,128)S(1)}, f32[2,256,128]{2,1,0:T(8,128)S(1)}, u32[]{:S(2)}, u32[]{:S(2)}) collective-permute-start(f32[2,256,128]{2,1,0:T(8,128)S(1)} %copy.28), channel_id=1, source_target_pairs={{0,8},{8,16},{16,24},{24,0},{1,9},{9,17},{17,25},{25,1},{2,10},{10... | collective-permute-start | bytes 786440 | tf_op jit(solution)/shard_map/ppermute | solution.py:15
  106.4 5.7 %collective-permute-start.14 = (f32[20,2,128]{2,0,1:T(8,128)S(1)}, f32[20,2,128]{2,0,1:T(8,128)S(1)}, u32[]{:S(2)}, u32[]{:S(2)}) collective-permute-start(f32[20,2,128]{2,0,1:T(8,128)S(1)} %get-tuple-element.15), channel_id=1, source_target_pairs={{0,2},{2,4},{4,6},{6,0},{1,3},{3,5},{5,7},{7,1},{8,10},{10,12},{12... | collective-permute-start | bytes 61448 | tf_op jit(solution)/shard_map/ppermute | solution.py:15
  106.4 5.6 %collective-permute-start.15 = (f32[20,2,128]{2,0,1:T(8,128)S(1)}, f32[20,2,128]{2,0,1:T(8,128)S(1)}, u32[]{:S(2)}, u32[]{:S(2)}) collective-permute-start(f32[20,2,128]{2,0,1:T(8,128)S(1)} %get-tuple-element.16), channel_id=1, source_target_pairs={{2,0},{4,2},{6,4},{0,6},{3,1},{5,3},{7,5},{1,7},{10,8},{12,10},{14... | collective-permute-start | bytes 61448 | tf_op jit(solution)/shard_map/ppermute | solution.py:18
  120.4 5.9 %collective-permute-start.16 = (f32[20,260,2]{1,0,2:T(8,128)S(1)}, f32[20,260,2]{1,0,2:T(8,128)S(1)}, u32[]{:S(2)}, u32[]{:S(2)}) collective-permute-start(f32[20,260,2]{1,0,2:T(8,128)S(1)} %copy.32), channel_id=1, source_target_pairs={{0,1},{1,0},{2,3},{3,2},{4,5},{5,4},{6,7},{7,6},{8,9},{9,8},{10,11... | collective-permute-start | bytes 124808 | tf_op jit(solution)/shard_map/ppermute | solution.py:15
  125.9 4.4 %collective-permute-start.17 = (f32[20,260,2]{1,0,2:T(8,128)S(1)}, f32[20,260,2]{1,0,2:T(8,128)S(1)}, u32[]{:S(2)}, u32[]{:S(2)}) collective-permute-start(f32[20,260,2]{1,0,2:T(8,128)S(1)} %copy.33), channel_id=1, source_target_pairs={{1,0},{0,1},{3,2},{2,3},{5,4},{4,5},{7,6},{6,7},{9,8},{8,9},{11,10... | collective-permute-start | bytes 124808 | tf_op jit(solution)/shard_map/ppermute | solution.py:18
  167.1 6.7 %collective-permute-start.19 = (f32[2,256,128]{2,1,0:T(8,128)S(1)}, f32[2,256,128]{2,1,0:T(8,128)S(1)}, u32[]{:S(2)}, u32[]{:S(2)}) collective-permute-start(f32[2,256,128]{2,1,0:T(8,128)S(1)} %copy.38), channel_id=1, source_target_pairs={{8,0},{16,8},{24,16},{0,24},{9,1},{17,9},{25,17},{1,25},{10,2},{18... | collective-permute-start | bytes 786440 | tf_op jit(solution)/shard_map/ppermute | solution.py:18
  167.1 7.7 %collective-permute-start.18 = (f32[2,256,128]{2,1,0:T(8,128)S(1)}, f32[2,256,128]{2,1,0:T(8,128)S(1)}, u32[]{:S(2)}, u32[]{:S(2)}) collective-permute-start(f32[2,256,128]{2,1,0:T(8,128)S(1)} %copy.37), channel_id=1, source_target_pairs={{0,8},{8,16},{16,24},{24,0},{1,9},{9,17},{17,25},{25,1},{2,10},{10... | collective-permute-start | bytes 786440 | tf_op jit(solution)/shard_map/ppermute | solution.py:15
  175.0 5.8 %collective-permute-start.20 = (f32[20,2,128]{2,0,1:T(8,128)S(1)}, f32[20,2,128]{2,0,1:T(8,128)S(1)}, u32[]{:S(2)}, u32[]{:S(2)}) collective-permute-start(f32[20,2,128]{2,0,1:T(8,128)S(1)} %get-tuple-element.13), channel_id=1, source_target_pairs={{0,2},{2,4},{4,6},{6,0},{1,3},{3,5},{5,7},{7,1},{8,10},{10,12},{12... | collective-permute-start | bytes 61448 | tf_op jit(solution)/shard_map/ppermute | solution.py:15
  175.1 5.8 %collective-permute-start.21 = (f32[20,2,128]{2,0,1:T(8,128)S(1)}, f32[20,2,128]{2,0,1:T(8,128)S(1)}, u32[]{:S(2)}, u32[]{:S(2)}) collective-permute-start(f32[20,2,128]{2,0,1:T(8,128)S(1)} %get-tuple-element.14), channel_id=1, source_target_pairs={{2,0},{4,2},{6,4},{0,6},{3,1},{5,3},{7,5},{1,7},{10,8},{12,10},{14... | collective-permute-start | bytes 61448 | tf_op jit(solution)/shard_map/ppermute | solution.py:18
  189.0 5.9 %collective-permute-start.22 = (f32[20,260,2]{1,0,2:T(8,128)S(1)}, f32[20,260,2]{1,0,2:T(8,128)S(1)}, u32[]{:S(2)}, u32[]{:S(2)}) collective-permute-start(f32[20,260,2]{1,0,2:T(8,128)S(1)} %copy.41), channel_id=1, source_target_pairs={{0,1},{1,0},{2,3},{3,2},{4,5},{5,4},{6,7},{7,6},{8,9},{9,8},{10,11... | collective-permute-start | bytes 124808 | tf_op jit(solution)/shard_map/ppermute | solution.py:15
  194.0 4.4 %collective-permute-start.23 = (f32[20,260,2]{1,0,2:T(8,128)S(1)}, f32[20,260,2]{1,0,2:T(8,128)S(1)}, u32[]{:S(2)}, u32[]{:S(2)}) collective-permute-start(f32[20,260,2]{1,0,2:T(8,128)S(1)} %copy.42), channel_id=1, source_target_pairs={{1,0},{0,1},{3,2},{2,3},{5,4},{4,5},{7,6},{6,7},{9,8},{8,9},{11,10... | collective-permute-start | bytes 124808 | tf_op jit(solution)/shard_map/ppermute | solution.py:18
  (4 other events, 35.8 us)
where the time goes:
time: 241 us; the launch traced here: 237 us
  other arithmetic  103 us (43%)
  local copies, waits for them, and re-layouts  83.9 us (35%)
  starting transfers between devices  30.6 us (13%)
  waiting for transfers between devices  19.5 us (8%)
    mul x3, other arithmetic, on_device(): jnp.where(parity_ext == 0, (source_ext + neighbours(padded)) / 6.0, exten...  55.5 us
    slice x14, local copies, waits for them, and re-layouts, extended_2(): lax.slice_in_dim(block, block.shape[dim] - width, None, axis=dim)  33.4 us
    mul x3, other arithmetic, on_device(): extended_2(values, (('gx', 0), ('gy', 1), ('gz', 2)), 2) * wide_walls  26.6 us
    ppermute x12, starting transfers between devices, extended_2(): lax.ppermute(lax.slice_in_dim(block, 0, width, axis=dim), axis, backward)  20.4 us
    select_n x3, other arithmetic, on_device(): jnp.where(parity == 1, (source + neighbours(extended)) / 6.0, extended[1:...  16.9 us
    slice x6, local copies, waits for them, and re-layouts, extended_2(): lax.slice_in_dim(block, 0, width, axis=dim)  15 us
    ppermute x7, local copies, waits for them, and re-layouts, extended_2(): lax.ppermute(lax.slice_in_dim(block, block.shape[dim] - width, None, axis...  14.8 us
    ppermute x7, local copies, waits for them, and re-layouts, extended_2(): lax.ppermute(lax.slice_in_dim(block, 0, width, axis=dim), axis, backward)  14.8 us
  transfers between devices with their start and end apart: 24, of which 8 were waited for; matrix products, arithmetic and copies ran while one was open for 24% of the time, Pallas kernels for 0%

commit v1 on v0

v1 whole, which is shorter than its diff:
```python
import functools

import jax
import jax.numpy as jnp
from jax import lax
from jax.experimental import pallas as pl
from jax.experimental.pallas import tpu as pltpu
from jax.sharding import PartitionSpec as P

SWEEPS = 3
MESH = pl.DeviceIdType.MESH
GROUP = 8
PAD = 8
X_LO, X_HI, Y_LO, Y_HI, Z_LO, Z_HI = range(6)


def kernel(sizes, f_hbm, s_hbm, o_hbm, fv, sv, ov, x, src, comb, kb, kr, jb, jr, ib, ir, send, recv, fsem, ssem, osem):
    ngx, ngy, ngz = sizes
    planes, rows, cols = f_hbm.shape
    nm = planes // 2
    half = rows // 2
    per_plane = rows // 8
    rounds = 2 * SWEEPS
    gx, gy, gz = (lax.axis_index(a) for a in ("gx", "gy", "gz"))
    has_lo, has_hi = gx > 0, gx < ngx - 1
    one_z = ngz == 2
    y_lo, y_hi = lax.rem(gy + ngy - 1, ngy), lax.rem(gy + 1, ngy)
    z_lo, z_hi = lax.rem(gz + ngz - 1, ngz), lax.rem(gz + 1, ngz)
    order = [0, nm - 1] + list(range(1, nm - 1))

    def load(ref, to, sem, m):
        return pltpu.make_async_copy(ref.at[pl.ds(2 * m, 2)], to.at[pl.ds(2 * m, 2)], sem.at[m])

    for m in order:
        load(f_hbm, fv, fsem, m).start()
    for m in order:
        load(s_hbm, sv, ssem, m).start()

    barrier = pltpu.get_barrier_semaphore()

    def greet(device):
        pl.semaphore_signal(barrier, inc=1, device_id=device, device_id_type=MESH)

    @pl.when(has_lo)
    def _():
        greet({"gx": gx - 1})

    @pl.when(has_hi)
    def _():
        greet({"gx": gx + 1})

    ys = [y_lo] if ngy == 2 else [y_lo, y_hi]
    zs = [z_lo] if one_z else [z_lo, z_hi]
    for y in ys:
        greet({"gy": y})
    for z in zs:
        greet({"gz": z})

    row8 = lax.broadcasted_iota(jnp.int32, (8, cols), 0)
    lane = lax.broadcasted_iota(jnp.int32, (8, cols), 1)
    odd8 = lax.rem(row8 + lane, 2)
    pair8 = lax.div(lane, 2)
    odd3 = jnp.broadcast_to(odd8[None], (GROUP, 8, cols)) == 1
    first3 = jnp.broadcast_to(lane[None], (GROUP, 8, cols)) == 0
    last3 = jnp.broadcast_to(lane[None], (GROUP, 8, cols)) == cols - 1
    even_lane = lax.rem(lane, 2) == 0
    odd_lane_half = lax.rem(lax.broadcasted_iota(jnp.int32, (half, cols), 1), 2) == 1

    zero = jnp.zeros((rows, cols), jnp.float32)

    @pl.when(jnp.logical_not(has_lo))
    def _():
        for c in range(2):
            x[c, 0, pl.ds(PAD, rows), :] = zero

    @pl.when(jnp.logical_not(has_hi))
    def _():
        for c in range(2):
            x[c, nm + 1, pl.ds(PAD, rows), :] = zero

    def three(v):
        return v.reshape(GROUP, 8, cols)

    def flat(v):
        return v.reshape(GROUP * 8, cols)

    def pair(produce, store, a, members, pack_to):
        acc = jnp.zeros((8, cols), jnp.float32)
        for h, m in enumerate(members):
            for blk in range(per_plane // GROUP):
                start = blk * GROUP * 8
                y = produce(a, m, h * per_plane + blk * GROUP, start)
                store(m, start, y)
                if pack_to is not None:
                    for g in range(GROUP):
                        q = h * per_plane + blk * GROUP + g
                        acc = jnp.where(pair8 == q, pltpu.roll(y[g], (2 * q + 1) % cols, 1), acc)
        if pack_to is not None:
            pack_to[a] = acc

    def inner(produce, store, pack_to):
        def body(a, carry):
            pair(produce, store, a, (1 + 2 * a, 2 + 2 * a), pack_to)
            return carry

        lax.fori_loop(0, nm // 2 - 1, body, 0)

    def outer(produce, store, pack_to):
        pair(produce, store, nm // 2 - 1, (0, nm - 1), pack_to)

    def copy(src_ref, dst_ref, to, t, out_dir, in_dir):
        return pltpu.make_async_remote_copy(
            src_ref=src_ref, dst_ref=dst_ref, send_sem=send.at[out_dir, t], recv_sem=recv.at[in_dir, t],
            device_id=to, device_id_type=MESH,
        )

    def x_lo_copy(t):
        return copy(ib.at[0, t], ir.at[1, t], {"gx": gx - 1}, t, X_LO, X_HI)

    def x_hi_copy(t):
        return copy(ib.at[1, t], ir.at[0, t], {"gx": gx + 1}, t, X_HI, X_LO)

    def y_copies(t):
        return (
            copy(jb.at[0, t], jr.at[1, t], {"gy": y_lo}, t, Y_LO, Y_HI),
            copy(jb.at[1, t], jr.at[0, t], {"gy": y_hi}, t, Y_HI, Y_LO),
        )

    def z_copies(t):
        up = copy(kb.at[t], kr.at[0, t], {"gz": z_hi}, t, Z_HI, Z_LO)
        if one_z:
            return (up,)
        return (up, copy(kb.at[t], kr.at[1, t], {"gz": z_lo}, t, Z_LO, Z_HI))

    def face(c, side):
        m = 1 if side == 0 else nm
        even = x[c, m, pl.ds(PAD, half, stride=2), :]
        odd = x[c, m, pl.ds(PAD + 1, half, stride=2), :]
        wanted = c if side == 0 else 1 - c
        return jnp.where(odd_lane_half, even, odd) if wanted == 1 else jnp.where(odd_lane_half, odd, even)

    def send_x(c, t):
        @pl.when(has_lo)
        def _():
            ib[0, t] = face(c, 0)
            x_lo_copy(t).start()

        @pl.when(has_hi)
        def _():
            ib[1, t] = face(c, 1)
            x_hi_copy(t).start()

    def send_yz(c, t):
        for z in z_copies(t):
            z.start()
        for m in range(nm):
            jb[0, t, pl.ds(m, 1), :] = x[c, m + 1, pl.ds(PAD, 1), :]
            jb[1, t, pl.ds(m, 1), :] = x[c, m + 1, pl.ds(PAD + rows - 1, 1), :]
        for y in y_copies(t):
            y.start()

    def take_yz(c, t):
        for z in z_copies(t):
            z.wait_recv()
        for a in range(nm // 2):
            low = kr[0, t, a]
            high = low if one_z else kr[1, t, a]
            comb[t, a] = jnp.where(even_lane, pltpu.roll(high, cols - 1, 1), pltpu.roll(low, 1, 1))
        for y in y_copies(t):
            y.wait_recv()
        for m in range(nm):
            x[c, m + 1, pl.ds(PAD - 1, 1), :] = jr[0, t, pl.ds(m, 1), :]
            x[c, m + 1, pl.ds(PAD + rows, 1), :] = jr[1, t, pl.ds(m, 1), :]

    def take_x(c, t):
        @pl.when(has_lo)
        def _():
            x_hi_copy_in = copy(ib.at[1, t], ir.at[0, t], {"gx": gx - 1}, t, X_HI, X_LO)
            x_hi_copy_in.wait_recv()
            got = ir[0, t]
            x[c, 0, pl.ds(PAD, half, stride=2), :] = got
            x[c, 0, pl.ds(PAD + 1, half, stride=2), :] = got

        @pl.when(has_hi)
        def _():
            x_lo_copy_in = copy(ib.at[0, t], ir.at[1, t], {"gx": gx + 1}, t, X_LO, X_HI)
            x_lo_copy_in.wait_recv()
            got = ir[1, t]
            x[c, nm + 1, pl.ds(PAD, half, stride=2), :] = got
            x[c, nm + 1, pl.ds(PAD + 1, half, stride=2), :] = got

    def store_to(c):
        def store(m, start, y):
            x[c, m + 1, pl.ds(PAD + start, GROUP * 8), :] = flat(y)

        return store

    def black_of_field(a, m, q0, start):
        low = three(fv[2 * m, pl.ds(start, GROUP * 8), :])
        high = three(fv[2 * m + 1, pl.ds(start, GROUP * 8), :])
        return jnp.where(odd3, low, high)

    for m in (0, nm - 1):
        load(f_hbm, fv, fsem, m).wait()
    pl.semaphore_wait(barrier, len(ys) + len(zs) + has_lo.astype(jnp.int32) + has_hi.astype(jnp.int32))
    outer(black_of_field, store_to(1), kb.at[0])
    send_x(1, 0)
    for m in range(1, nm - 1):
        load(f_hbm, fv, fsem, m).wait()
    inner(black_of_field, store_to(1), kb.at[0])
    send_yz(1, 0)

    for m in order:
        load(s_hbm, sv, ssem, m).wait()

    def split_source(m, carry):
        for blk in range(per_plane // GROUP):
            rs = pl.ds(blk * GROUP * 8, GROUP * 8)
            low, high = three(sv[2 * m, rs, :]), three(sv[2 * m + 1, rs, :])
            src[0, m, rs, :] = flat(jnp.where(odd3, high, low))
            src[1, m, rs, :] = flat(jnp.where(odd3, low, high))
        return carry

    lax.fori_loop(0, nm, split_source, 0)

    def relax(c, t):
        d = 1 - c

        def produce(a, m, q0, start):
            rs = pl.ds(PAD + start, GROUP * 8)
            here = three(x[d, m + 1, rs, :])
            below, above = three(x[d, m, rs, :]), three(x[d, m + 2, rs, :])
            beside = jnp.where(odd3, above, below) if c == 0 else jnp.where(odd3, below, above)
            total = three(src[c, m, pl.ds(start, GROUP * 8), :]) + here + beside
            total = total + three(x[d, m + 1, pl.ds(PAD + start - 1, GROUP * 8), :])
            total = total + three(x[d, m + 1, pl.ds(PAD + start + 1, GROUP * 8), :])
            edges = comb[t, a]
            edge = jnp.stack(
                [pltpu.roll(edges, (2 * cols - (2 * (q0 + g) + 1)) % cols, 1) for g in range(GROUP)], axis=0
            )
            total = total + jnp.where(first3, edge, pltpu.roll(here, 1, 2))
            total = total + jnp.where(last3, edge, pltpu.roll(here, cols - 1, 2))
            return total * jnp.float32(1.0 / 6.0)

        return produce

    def out_copy(m):
        return pltpu.make_async_copy(ov.at[pl.ds(2 * m, 2)], o_hbm.at[pl.ds(2 * m, 2)], osem.at[m])

    def store_out(m, start, y):
        red = three(x[0, m + 1, pl.ds(PAD + start, GROUP * 8), :])
        rs = pl.ds(start, GROUP * 8)
        ov[2 * m, rs, :] = flat(jnp.where(odd3, y, red))
        ov[2 * m + 1, rs, :] = flat(jnp.where(odd3, red, y))

    for t in range(rounds):
        c = t % 2
        final = t == rounds - 1
        store = store_out if final else store_to(c)
        pack = None if final else kb.at[t + 1]
        take_yz(1 - c, t)
        inner(relax(c, t), store, pack)
        if final:
            for m in range(1, nm - 1):
                out_copy(m).start()
        take_x(1 - c, t)
        outer(relax(c, t), store, pack)
        if final:
            for m in (0, nm - 1):
                out_copy(m).start()
        else:
            send_x(c, t + 1)
            send_yz(c, t + 1)

    for t in range(rounds):
        for cp in z_copies(t) + y_copies(t):
            cp.wait_send()

        @pl.when(has_lo)
        def _():
            x_lo_copy(t).wait_send()

        @pl.when(has_hi)
        def _():
            x_hi_copy(t).wait_send()

    for m in range(nm):
        out_copy(m).wait()


def solution(mesh):
    sizes = tuple(mesh.shape[a] for a in ("gx", "gy", "gz"))

    def on_device(field, source):
        planes, rows, cols = field.shape
        nm, rounds = planes // 2, 2 * SWEEPS
        assert planes % 4 == 0 and rows % (8 * GROUP) == 0 and cols == 128 and rows // 2 == cols
        f32 = jnp.float32
        return pl.pallas_call(
            functools.partial(kernel, sizes),
            out_shape=jax.ShapeDtypeStruct(field.shape, f32),
            in_specs=[pl.BlockSpec(memory_space=pl.ANY)] * 2,
            out_specs=pl.BlockSpec(memory_space=pl.ANY),
            scratch_shapes=[
                pltpu.VMEM(field.shape, f32),
                pltpu.VMEM(field.shape, f32),
                pltpu.VMEM(field.shape, f32),
                pltpu.VMEM((2, nm + 2, rows + 2 * PAD, cols), f32),
                pltpu.VMEM((2, nm, rows, cols), f32),
                pltpu.VMEM((rounds, nm // 2, 8, cols), f32),
                pltpu.VMEM((rounds, nm // 2, 8, cols), f32),
                pltpu.VMEM((2, rounds, nm // 2, 8, cols), f32),
                pltpu.VMEM((2, rounds, nm, cols), f32),
                pltpu.VMEM((2, rounds, nm, cols), f32),
                pltpu.VMEM((2, rounds, rows // 2, cols), f32),
                pltpu.VMEM((2, rounds, rows // 2, cols), f32),
                pltpu.SemaphoreType.DMA((6, rounds)),
                pltpu.SemaphoreType.DMA((6, rounds)),
                pltpu.SemaphoreType.DMA((nm,)),
                pltpu.SemaphoreType.DMA((nm,)),
                pltpu.SemaphoreType.DMA((nm,)),
            ],
            compiler_params=pltpu.CompilerParams(
                collective_id=0, has_side_effects=True, vmem_limit_bytes=32 * 1024 * 1024
            ),
        )(field, source)

    spec = P("gx", "gy", "gz")
    return jax.shard_map(on_device, mesh=mesh, in_specs=(spec, spec), out_specs=spec, check_vma=False)
```

time: 241 us -> 46.4 us (0.19); the launches traced: 237 us -> 46.2 us
  other arithmetic: 103 us -> 0 us
  local copies, waits for them, and re-layouts: 83.9 us -> 4.5 us
  Pallas kernels: 0 us -> 41.7 us
  starting transfers between devices: 30.6 us -> 0 us
  waiting for transfers between devices: 19.5 us -> 0 us
    mul x6 -> x0, other arithmetic: 82.1 us -> none  [the longest x3 55.5 us: on_device(): jnp.where(parity_ext == 0, (source_ext + neighbours(padded)) / 6.0, exten...]
    slice x20 -> x0, local copies, waits for them, and re-layouts: 48.4 us -> none  [the longest x14 33.4 us: extended_2(): lax.slice_in_dim(block, block.shape[dim] - width, None, axis=dim)]
    pallas_call x0 -> x1, Pallas kernels: none -> 41.7 us  [on_device(): pl.pallas_call(functools.partial(kernel, sizes), out_shape=jax.ShapeDtype...]
    ppermute x24 -> x0, starting transfers between devices: 30.6 us -> none  [the longest x12 20.4 us: extended_2(): lax.ppermute(lax.slice_in_dim(block, 0, width, axis=dim), axis, backward)]
    ppermute x14 -> x0, local copies, waits for them, and re-layouts: 29.6 us -> none  [the longest x7 14.8 us: extended_2(): lax.ppermute(lax.slice_in_dim(block, block.shape[dim] - width, None, axis...]
    ppermute x24 -> x0, waiting for transfers between devices: 19.5 us -> none  [the longest x12 11.6 us: extended_2(): lax.ppermute(lax.slice_in_dim(block, 0, width, axis=dim), axis, backward)]
    select_n x5 -> x0, other arithmetic: 16.9 us -> none  [the longest x3 16.9 us: on_device(): jnp.where(parity == 1, (source + neighbours(extended)) / 6.0, extended[1:...]
    concatenate x4 -> x0, other arithmetic: 3.47 us -> none  [extended_2(): block = jnp.concatenate([low, block, high], axis=dim)]
  transfers between devices with their start and end apart: 24 -> 0, of which waited for: 8 -> 0; matrix products, arithmetic and copies ran while one was open for 24% -> 0% of each run, Pallas kernels for 0% -> 0%
where the time goes in v1:
time: 46.4 us; the launch traced here: 46.2 us
  Pallas kernels  41.7 us (90%)
  local copies, waits for them, and re-layouts  4.5 us (10%)
    pallas_call x1, Pallas kernels, on_device(): pl.pallas_call(functools.partial(kernel, sizes), out_shape=jax.ShapeDtype...  41.7 us
    unnamed x5, local copies, waits for them, and re-layouts  4.5 us

profile of v1, /device:TPU:0, one launch (start us, length us, event | category | flops | bytes accessed | tf_op | source)
XLA Modules:
  0.0 46.2 jit_solution(5480397166240940830)
XLA Ops:
  0.0 0.0 copy-start
  0.0 1.6 %copy-done = f32[16,256,128]{2,1,0:T(8,128)S(1)} copy-done((f32[16,256,128]{2,1,0:T(8,128)S(1)}, f32[16,256,128]{2,1,0:T(8,128)}, u32[]{:S(2)}) %copy-start) | copy-done | bytes 2097176
  1.6 0.0 copy-start.1
  1.6 1.6 %copy-done.1 = f32[16,256,128]{2,1,0:T(8,128)S(1)} copy-done((f32[16,256,128]{2,1,0:T(8,128)S(1)}, f32[16,256,128]{2,1,0:T(8,128)}, u32[]{:S(2)}) %copy-start.1) | copy-done | bytes 2097176
  3.2 41.7 %shard_map.28 = f32[16,256,128]{2,1,0:T(8,128)S(1)} custom-call(f32[16,256,128]{2,1,0:T(8,128)S(1)} %copy-done, f32[16,256,128]{2,1,0:T(8,128)S(1)} %copy-done.1), custom_call_target="tpu_custom_call" | custom-call | tf_op jit(solution)/shard_map/pallas_call | solution.py:299
  44.9 1.3 %copy.4 = f32[16,256,128]{2,1,0:T(8,128)} copy(f32[16,256,128]{2,1,0:T(8,128)S(1)} %shard_map.28) | data formatting | bytes 4194304
Async XLA Ops:
  0.0 1.6 %copy-start = (f32[16,256,128]{2,1,0:T(8,128)S(1)}, f32[16,256,128]{2,1,0:T(8,128)}, u32[]{:S(2)}) copy-start(f32[16,256,128]{2,1,0:T(8,128)} %f_hbm.1) | copy-start | bytes 6291460
  1.6 1.6 %copy-start.1 = (f32[16,256,128]{2,1,0:T(8,128)S(1)}, f32[16,256,128]{2,1,0:T(8,128)}, u32[]{:S(2)}) copy-start(f32[16,256,128]{2,1,0:T(8,128)} %s_hbm.1) | copy-start | bytes 6291460

commit v2 on v1

--- a/solution.py
+++ b/solution.py
@@ -14,7 +14,7 @@
 X_LO, X_HI, Y_LO, Y_HI, Z_LO, Z_HI = range(6)
 
 
-def kernel(sizes, f_hbm, s_hbm, o_hbm, fv, sv, ov, x, src, comb, kb, kr, jb, jr, ib, ir, send, recv, fsem, ssem, osem):
+def kernel(sizes, f_hbm, s_hbm, ov, fv, sv, x, src, comb, kb, kr, jb, jr, ib, ir, send, recv, fsem, ssem):
     ngx, ngy, ngz = sizes
     planes, rows, cols = f_hbm.shape
     nm = planes // 2
@@ -84,53 +84,47 @@
     def flat(v):
         return v.reshape(GROUP * 8, cols)
 
-    def pair(produce, store, a, members, pack_to):
-        acc = jnp.zeros((8, cols), jnp.float32)
-        for h, m in enumerate(members):
+    def pair(produce, store, a, pack_to):
+        accs = []
+        for h, m in enumerate((a, nm - 1 - a)):
             for blk in range(per_plane // GROUP):
                 start = blk * GROUP * 8
                 y = produce(a, m, h * per_plane + blk * GROUP, start)
                 store(m, start, y)
                 if pack_to is not None:
+                    acc = jnp.zeros((8, cols), jnp.float32)
                     for g in range(GROUP):
                         q = h * per_plane + blk * GROUP + g
                         acc = jnp.where(pair8 == q, pltpu.roll(y[g], (2 * q + 1) % cols, 1), acc)
+                    accs.append(acc)
         if pack_to is not None:
-            pack_to[a] = acc
-
-    def inner(produce, store, pack_to):
-        def body(a, carry):
-            pair(produce, store, a, (1 + 2 * a, 2 + 2 * a), pack_to)
-            return carry
-
-        lax.fori_loop(0, nm // 2 - 1, body, 0)
-
-    def outer(produce, store, pack_to):
-        pair(produce, store, nm // 2 - 1, (0, nm - 1), pack_to)
-
-    def copy(src_ref, dst_ref, to, t, out_dir, in_dir):
+            while len(accs) > 1:
+                accs = [p + q for p, q in zip(accs[::2], accs[1::2])]
+            pack_to[a] = accs[0]
+
+    def copy(src_ref, dst_ref, to, at, out_dir, in_dir):
         return pltpu.make_async_remote_copy(
-            src_ref=src_ref, dst_ref=dst_ref, send_sem=send.at[out_dir, t], recv_sem=recv.at[in_dir, t],
+            src_ref=src_ref, dst_ref=dst_ref, send_sem=send.at[(out_dir, *at)], recv_sem=recv.at[(in_dir, *at)],
             device_id=to, device_id_type=MESH,
         )
 
     def x_lo_copy(t):
-        return copy(ib.at[0, t], ir.at[1, t], {"gx": gx - 1}, t, X_LO, X_HI)
+        return copy(ib.at[0, t], ir.at[1, t], {"gx": gx - 1}, (t, 0), X_LO, X_HI)
 
     def x_hi_copy(t):
-        return copy(ib.at[1, t], ir.at[0, t], {"gx": gx + 1}, t, X_HI, X_LO)
-
-    def y_copies(t):
+        return copy(ib.at[1, t], ir.at[0, t], {"gx": gx + 1}, (t, 0), X_HI, X_LO)
+
+    def y_copies(t, a):
         return (
-            copy(jb.at[0, t], jr.at[1, t], {"gy": y_lo}, t, Y_LO, Y_HI),
-            copy(jb.at[1, t], jr.at[0, t], {"gy": y_hi}, t, Y_HI, Y_LO),
+            copy(jb.at[0, t, a], jr.at[1, t, a], {"gy": y_lo}, (t, a), Y_LO, Y_HI),
+            copy(jb.at[1, t, a], jr.at[0, t, a], {"gy": y_hi}, (t, a), Y_HI, Y_LO),
         )
 
-    def z_copies(t):
-        up = copy(kb.at[t], kr.at[0, t], {"gz": z_hi}, t, Z_HI, Z_LO)
+    def z_copies(t, a):
+        up = copy(kb.at[t, a], kr.at[0, t, a], {"gz": z_hi}, (t, a), Z_HI, Z_LO)
         if one_z:
             return (up,)
-        return (up, copy(kb.at[t], kr.at[1, t], {"gz": z_lo}, t, Z_LO, Z_HI))
+        return (up, copy(kb.at[t, a], kr.at[1, t, a], {"gz": z_lo}, (t, a), Z_LO, Z_HI))
 
     def face(c, side):
         m = 1 if side == 0 else nm
@@ -150,32 +144,31 @@
             ib[1, t] = face(c, 1)
             x_hi_copy(t).start()
 
-    def send_yz(c, t):
-        for z in z_copies(t):
+    def send_yz(c, t, a):
+        for z in z_copies(t, a):
             z.start()
-        for m in range(nm):
-            jb[0, t, pl.ds(m, 1), :] = x[c, m + 1, pl.ds(PAD, 1), :]
-            jb[1, t, pl.ds(m, 1), :] = x[c, m + 1, pl.ds(PAD + rows - 1, 1), :]
-        for y in y_copies(t):
+        for h, m in enumerate((a, nm - 1 - a)):
+            jb[0, t, a, pl.ds(h, 1), :] = x[c, m + 1, pl.ds(PAD, 1), :]
+            jb[1, t, a, pl.ds(h, 1), :] = x[c, m + 1, pl.ds(PAD + rows - 1, 1), :]
+        for y in y_copies(t, a):
             y.start()
 
-    def take_yz(c, t):
-        for z in z_copies(t):
+    def take_yz(c, t, a):
+        for z in z_copies(t, a):
             z.wait_recv()
-        for a in range(nm // 2):
-            low = kr[0, t, a]
-            high = low if one_z else kr[1, t, a]
-            comb[t, a] = jnp.where(even_lane, pltpu.roll(high, cols - 1, 1), pltpu.roll(low, 1, 1))
-        for y in y_copies(t):
+        low = kr[0, t, a]
+        high = low if one_z else kr[1, t, a]
+        comb[a] = jnp.where(even_lane, pltpu.roll(high, cols - 1, 1), pltpu.roll(low, 1, 1))
+        for y in y_copies(t, a):
             y.wait_recv()
-        for m in range(nm):
-            x[c, m + 1, pl.ds(PAD - 1, 1), :] = jr[0, t, pl.ds(m, 1), :]
-            x[c, m + 1, pl.ds(PAD + rows, 1), :] = jr[1, t, pl.ds(m, 1), :]
+        for h, m in enumerate((a, nm - 1 - a)):
+            x[c, m + 1, pl.ds(PAD - 1, 1), :] = jr[0, t, a, pl.ds(h, 1), :]
+            x[c, m + 1, pl.ds(PAD + rows, 1), :] = jr[1, t, a, pl.ds(h, 1), :]
 
     def take_x(c, t):
         @pl.when(has_lo)
         def _():
-            x_hi_copy_in = copy(ib.at[1, t], ir.at[0, t], {"gx": gx - 1}, t, X_HI, X_LO)
+            x_hi_copy_in = copy(ib.at[1, t], ir.at[0, t], {"gx": gx - 1}, (t, 0), X_HI, X_LO)
             x_hi_copy_in.wait_recv()
             got = ir[0, t]
             x[c, 0, pl.ds(PAD, half, stride=2), :] = got
@@ -183,7 +176,7 @@
 
         @pl.when(has_hi)
         def _():
-            x_lo_copy_in = copy(ib.at[0, t], ir.at[1, t], {"gx": gx + 1}, t, X_LO, X_HI)
+            x_lo_copy_in = copy(ib.at[0, t], ir.at[1, t], {"gx": gx + 1}, (t, 0), X_LO, X_HI)
             x_lo_copy_in.wait_recv()
             got = ir[1, t]
             x[c, nm + 1, pl.ds(PAD, half, stride=2), :] = got
@@ -203,12 +196,18 @@
     for m in (0, nm - 1):
         load(f_hbm, fv, fsem, m).wait()
     pl.semaphore_wait(barrier, len(ys) + len(zs) + has_lo.astype(jnp.int32) + has_hi.astype(jnp.int32))
-    outer(black_of_field, store_to(1), kb.at[0])
+    pair(black_of_field, store_to(1), 0, kb.at[0])
     send_x(1, 0)
-    for m in range(1, nm - 1):
-        load(f_hbm, fv, fsem, m).wait()
-    inner(black_of_field, store_to(1), kb.at[0])
-    send_yz(1, 0)
+    send_yz(1, 0, 0)
+
+    def first(a, carry):
+        for m in (a, nm - 1 - a):
+            load(f_hbm, fv, fsem, m).wait()
+        pair(black_of_field, store_to(1), a, kb.at[0])
+        send_yz(1, 0, a)
+        return carry
+
+    lax.fori_loop(1, nm // 2, first, 0)
 
     for m in order:
         load(s_hbm, sv, ssem, m).wait()
@@ -234,7 +233,7 @@
             total = three(src[c, m, pl.ds(start, GROUP * 8), :]) + here + beside
             total = total + three(x[d, m + 1, pl.ds(PAD + start - 1, GROUP * 8), :])
             total = total + three(x[d, m + 1, pl.ds(PAD + start + 1, GROUP * 8), :])
-            edges = comb[t, a]
+            edges = comb[a]
             edge = jnp.stack(
                 [pltpu.roll(edges, (2 * cols - (2 * (q0 + g) + 1)) % cols, 1) for g in range(GROUP)], axis=0
             )
@@ -244,9 +243,6 @@
 
         return produce
 
-    def out_copy(m):
-        return pltpu.make_async_copy(ov.at[pl.ds(2 * m, 2)], o_hbm.at[pl.ds(2 * m, 2)], osem.at[m])
-
     def store_out(m, start, y):
         red = three(x[0, m + 1, pl.ds(PAD + start, GROUP * 8), :])
         rs = pl.ds(start, GROUP * 8)
@@ -258,23 +254,28 @@
         final = t == rounds - 1
         store = store_out if final else store_to(c)
         pack = None if final else kb.at[t + 1]
-        take_yz(1 - c, t)
-        inner(relax(c, t), store, pack)
-        if final:
-            for m in range(1, nm - 1):
-                out_copy(m).start()
-        take_x(1 - c, t)
-        outer(relax(c, t), store, pack)
-        if final:
-            for m in (0, nm - 1):
-                out_copy(m).start()
-        else:
-            send_x(c, t + 1)
-            send_yz(c, t + 1)
+
+        def piece(a, first=False):
+            take_yz(1 - c, t, a)
+            if first:
+                take_x(1 - c, t)
+            pair(relax(c, t), store, a, pack)
+            if not final:
+                if first:
+                    send_x(c, t + 1)
+                send_yz(c, t + 1, a)
+
+        def body(a, carry):
+            piece(a)
+            return carry
+
+        piece(0, True)
+        lax.fori_loop(1, nm // 2, body, 0)
 
     for t in range(rounds):
-        for cp in z_copies(t) + y_copies(t):
-            cp.wait_send()
+        for a in range(nm // 2):
+            for cp in z_copies(t, a) + y_copies(t, a):
+                cp.wait_send()
 
         @pl.when(has_lo)
         def _():
@@ -283,9 +284,6 @@
         @pl.when(has_hi)
         def _():
             x_hi_copy(t).wait_send()
-
-    for m in range(nm):
-        out_copy(m).wait()
 
 
 def solution(mesh):
@@ -299,29 +297,27 @@
         return pl.pallas_call(
             functools.partial(kernel, sizes),
             out_shape=jax.ShapeDtypeStruct(field.shape, f32),
-            in_specs=[pl.BlockSpec(memory_space=pl.ANY)] * 2,
-            out_specs=pl.BlockSpec(memory_space=pl.ANY),
+            in_specs=[pl.BlockSpec(memory_space=pltpu.HBM)] * 2,
+            out_specs=pl.BlockSpec(memory_space=pltpu.VMEM),
             scratch_shapes=[
-                pltpu.VMEM(field.shape, f32),
                 pltpu.VMEM(field.shape, f32),
                 pltpu.VMEM(field.shape, f32),
                 pltpu.VMEM((2, nm + 2, rows + 2 * PAD, cols), f32),
                 pltpu.VMEM((2, nm, rows, cols), f32),
-                pltpu.VMEM((rounds, nm // 2, 8, cols), f32),
+                pltpu.VMEM((nm // 2, 8, cols), f32),
                 pltpu.VMEM((rounds, nm // 2, 8, cols), f32),
                 pltpu.VMEM((2, rounds, nm // 2, 8, cols), f32),
-                pltpu.VMEM((2, rounds, nm, cols), f32),
-                pltpu.VMEM((2, rounds, nm, cols), f32),
+                pltpu.VMEM((2, rounds, nm // 2, 2, cols), f32),
+                pltpu.VMEM((2, rounds, nm // 2, 2, cols), f32),
                 pltpu.VMEM((2, rounds, rows // 2, cols), f32),
                 pltpu.VMEM((2, rounds, rows // 2, cols), f32),
-                pltpu.SemaphoreType.DMA((6, rounds)),
-                pltpu.SemaphoreType.DMA((6, rounds)),
-                pltpu.SemaphoreType.DMA((nm,)),
+                pltpu.SemaphoreType.DMA((6, rounds, nm // 2)),
+                pltpu.SemaphoreType.DMA((6, rounds, nm // 2)),
                 pltpu.SemaphoreType.DMA((nm,)),
                 pltpu.SemaphoreType.DMA((nm,)),
             ],
             compiler_params=pltpu.CompilerParams(
-                collective_id=0, has_side_effects=True, vmem_limit_bytes=32 * 1024 * 1024
+                collective_id=0, has_side_effects=True, vmem_limit_bytes=60 * 1024 * 1024
             ),
         )(field, source)
 

time: 46.4 us -> 39 us (0.84)
  Pallas kernels: 41.7 us -> 35.8 us
  local copies, waits for them, and re-layouts: 4.5 us -> 3.11 us
    pallas_call x1, Pallas kernels: 41.7 us -> 35.8 us  [on_device(): pl.pallas_call(functools.partial(kernel, sizes), out_shape=jax.ShapeDtype...]
    unnamed x5 -> x1, local copies, waits for them, and re-layouts: 4.5 us -> 3.11 us
where the time goes in v2:
time: 39 us; the launch traced here: 38.9 us
  Pallas kernels  35.8 us (92%)
  local copies, waits for them, and re-layouts  3.11 us (8%)
    pallas_call x1, Pallas kernels, on_device(): pl.pallas_call(functools.partial(kernel, sizes), out_shape=jax.ShapeDtype...  35.8 us
    unnamed x1, local copies, waits for them, and re-layouts  3.11 us

profile of v2, /device:TPU:0, one launch (start us, length us, event | category | flops | bytes accessed | tf_op | source)
XLA Modules:
  0.0 38.9 jit_solution(1518617081810871570)
XLA Ops:
  0.0 35.8 %shard_map.28 = f32[16,256,128]{2,1,0:T(8,128)} custom-call(f32[16,256,128]{2,1,0:T(8,128)} %f_hbm.1, f32[16,256,128]{2,1,0:T(8,128)} %s_hbm.1), custom_call_target="tpu_custom_call" | custom-call | tf_op jit(solution)/shard_map/pallas_call | solution.py:297
  35.8 3.1 %copy.4 = f32[16,256,128]{2,1,0:T(8,128)} copy(f32[16,256,128]{2,1,0:T(8,128)} %shard_map.28) | data formatting | bytes 4194304

commit v3 on v2

--- a/solution.py
+++ b/solution.py
@@ -9,7 +9,7 @@
 
 SWEEPS = 3
 MESH = pl.DeviceIdType.MESH
-GROUP = 8
+GROUP = 32
 PAD = 8
 X_LO, X_HI, Y_LO, Y_HI, Z_LO, Z_HI = range(6)
 
@@ -26,7 +26,7 @@
     one_z = ngz == 2
     y_lo, y_hi = lax.rem(gy + ngy - 1, ngy), lax.rem(gy + 1, ngy)
     z_lo, z_hi = lax.rem(gz + ngz - 1, ngz), lax.rem(gz + 1, ngz)
-    order = [0, nm - 1] + list(range(1, nm - 1))
+    order = [m for a in range(nm // 2) for m in (a, nm - 1 - a)]
 
     def load(ref, to, sem, m):
         return pltpu.make_async_copy(ref.at[pl.ds(2 * m, 2)], to.at[pl.ds(2 * m, 2)], sem.at[m])
@@ -193,24 +193,11 @@
         high = three(fv[2 * m + 1, pl.ds(start, GROUP * 8), :])
         return jnp.where(odd3, low, high)
 
-    for m in (0, nm - 1):
-        load(f_hbm, fv, fsem, m).wait()
-    pl.semaphore_wait(barrier, len(ys) + len(zs) + has_lo.astype(jnp.int32) + has_hi.astype(jnp.int32))
-    pair(black_of_field, store_to(1), 0, kb.at[0])
-    send_x(1, 0)
-    send_yz(1, 0, 0)
-
-    def first(a, carry):
+    def pack_field(a, carry):
         for m in (a, nm - 1 - a):
             load(f_hbm, fv, fsem, m).wait()
         pair(black_of_field, store_to(1), a, kb.at[0])
-        send_yz(1, 0, a)
         return carry
-
-    lax.fori_loop(1, nm // 2, first, 0)
-
-    for m in order:
-        load(s_hbm, sv, ssem, m).wait()
 
     def split_source(m, carry):
         for blk in range(per_plane // GROUP):
@@ -220,7 +207,18 @@
             src[1, m, rs, :] = flat(jnp.where(odd3, low, high))
         return carry
 
-    lax.fori_loop(0, nm, split_source, 0)
+    def split_pair(a, carry):
+        for m in (a, nm - 1 - a):
+            load(s_hbm, sv, ssem, m).wait()
+            split_source(m, 0)
+        return carry
+
+    lax.fori_loop(0, nm // 2, pack_field, 0)
+    lax.fori_loop(0, nm // 2, split_pair, 0)
+    pl.semaphore_wait(barrier, len(ys) + len(zs) + has_lo.astype(jnp.int32) + has_hi.astype(jnp.int32))
+    send_x(1, 0)
+    for a in range(nm // 2):
+        send_yz(1, 0, a)
 
     def relax(c, t):
         d = 1 - c
@@ -317,7 +315,7 @@
                 pltpu.SemaphoreType.DMA((nm,)),
             ],
             compiler_params=pltpu.CompilerParams(
-                collective_id=0, has_side_effects=True, vmem_limit_bytes=60 * 1024 * 1024
+                collective_id=0, has_side_effects=True, vmem_limit_bytes=50 * 1024 * 1024
             ),
         )(field, source)
 

time: 39 us -> 34.5 us (0.88)
  Pallas kernels: 35.8 us -> 33 us
  local copies, waits for them, and re-layouts: 3.11 us -> 1.32 us
    pallas_call x1, Pallas kernels: 35.8 us -> 33 us  [on_device(): pl.pallas_call(functools.partial(kernel, sizes), out_shape=jax.ShapeDtype...]
    unnamed x1, local copies, waits for them, and re-layouts: 3.11 us -> 1.32 us
where the time goes in v3:
time: 34.5 us; the launch traced here: 34.4 us
  Pallas kernels  33 us (96%)
  local copies, waits for them, and re-layouts  1.32 us (4%)
    pallas_call x1, Pallas kernels, on_device(): pl.pallas_call(functools.partial(kernel, sizes), out_shape=jax.ShapeDtype...  33 us
    unnamed x1, local copies, waits for them, and re-layouts  1.32 us

profile of v3, /device:TPU:0, one launch (start us, length us, event | category | flops | bytes accessed | tf_op | source)
XLA Modules:
  0.0 34.4 jit_solution(16404968973763476017)
XLA Ops:
  0.0 33.0 %shard_map.28 = f32[16,256,128]{2,1,0:T(8,128)S(1)} custom-call(f32[16,256,128]{2,1,0:T(8,128)} %f_hbm.1, f32[16,256,128]{2,1,0:T(8,128)} %s_hbm.1), custom_call_target="tpu_custom_call" | custom-call | tf_op jit(solution)/shard_map/pallas_call | solution.py:295
  33.0 1.3 %copy.4 = f32[16,256,128]{2,1,0:T(8,128)} copy(f32[16,256,128]{2,1,0:T(8,128)S(1)} %shard_map.28) | data formatting | bytes 4194304

commit v4 on v3

--- a/solution.py
+++ b/solution.py
@@ -144,12 +144,15 @@
             ib[1, t] = face(c, 1)
             x_hi_copy(t).start()
 
-    def send_yz(c, t, a):
+    def send_z(t, a):
         for z in z_copies(t, a):
             z.start()
+
+    def send_y(t, a, outermost):
         for h, m in enumerate((a, nm - 1 - a)):
-            jb[0, t, a, pl.ds(h, 1), :] = x[c, m + 1, pl.ds(PAD, 1), :]
-            jb[1, t, a, pl.ds(h, 1), :] = x[c, m + 1, pl.ds(PAD + rows - 1, 1), :]
+            low, high = outermost(a, m, h)
+            jb[0, t, a, pl.ds(h, 1), :] = low
+            jb[1, t, a, pl.ds(h, 1), :] = high
         for y in y_copies(t, a):
             y.start()
 
@@ -217,8 +220,13 @@
     lax.fori_loop(0, nm // 2, split_pair, 0)
     pl.semaphore_wait(barrier, len(ys) + len(zs) + has_lo.astype(jnp.int32) + has_hi.astype(jnp.int32))
     send_x(1, 0)
+
+    def stored_rows(a, m, h):
+        return x[1, m + 1, pl.ds(PAD, 1), :], x[1, m + 1, pl.ds(PAD + rows - 1, 1), :]
+
     for a in range(nm // 2):
-        send_yz(1, 0, a)
+        send_y(0, a, stored_rows)
+        send_z(0, a)
 
     def relax(c, t):
         d = 1 - c
@@ -241,6 +249,28 @@
 
         return produce
 
+    def early_rows(c):
+        d = 1 - c
+
+        def tile(a, m, q, start):
+            rs = pl.ds(PAD + start, 8)
+            here = x[d, m + 1, rs, :]
+            below, above = x[d, m, rs, :], x[d, m + 2, rs, :]
+            beside = jnp.where(odd8 == 1, above, below) if c == 0 else jnp.where(odd8 == 1, below, above)
+            total = src[c, m, pl.ds(start, 8), :] + here + beside
+            total = total + x[d, m + 1, pl.ds(PAD + start - 1, 8), :]
+            total = total + x[d, m + 1, pl.ds(PAD + start + 1, 8), :]
+            edge = pltpu.roll(comb[a], (2 * cols - (2 * q + 1)) % cols, 1)
+            total = total + jnp.where(lane == 0, edge, pltpu.roll(here, 1, 1))
+            total = total + jnp.where(lane == cols - 1, edge, pltpu.roll(here, cols - 1, 1))
+            return total * jnp.float32(1.0 / 6.0)
+
+        def outermost(a, m, h):
+            q = h * per_plane
+            return tile(a, m, q, 0)[0:1], tile(a, m, q + per_plane - 1, rows - 8)[7:8]
+
+        return outermost
+
     def store_out(m, start, y):
         red = three(x[0, m + 1, pl.ds(PAD + start, GROUP * 8), :])
         rs = pl.ds(start, GROUP * 8)
@@ -257,11 +287,13 @@
             take_yz(1 - c, t, a)
             if first:
                 take_x(1 - c, t)
+            if not final:
+                send_y(t + 1, a, early_rows(c))
             pair(relax(c, t), store, a, pack)
             if not final:
                 if first:
                     send_x(c, t + 1)
-                send_yz(c, t + 1, a)
+                send_z(t + 1, a)
 
         def body(a, carry):
             piece(a)

time: 34.5 us -> 33.4 us (0.968)
  Pallas kernels: 33 us -> 31.9 us
    pallas_call x1, Pallas kernels: 33 us -> 31.9 us  [on_device(): pl.pallas_call(functools.partial(kernel, sizes), out_shape=jax.ShapeDtype...]
where the time goes in v4:
time: 33.4 us; the launch traced here: 33.2 us
  Pallas kernels  31.9 us (96%)
  local copies, waits for them, and re-layouts  1.32 us (4%)
    pallas_call x1, Pallas kernels, on_device(): pl.pallas_call(functools.partial(kernel, sizes), out_shape=jax.ShapeDtype...  31.9 us
    unnamed x1, local copies, waits for them, and re-layouts  1.32 us

profile of v4, /device:TPU:0, one launch (start us, length us, event | category | flops | bytes accessed | tf_op | source)
XLA Modules:
  0.0 33.2 jit_solution(8849381412353959836)
XLA Ops:
  0.0 31.9 %shard_map.28 = f32[16,256,128]{2,1,0:T(8,128)S(1)} custom-call(f32[16,256,128]{2,1,0:T(8,128)} %f_hbm.1, f32[16,256,128]{2,1,0:T(8,128)} %s_hbm.1), custom_call_target="tpu_custom_call" | custom-call | tf_op jit(solution)/shard_map/pallas_call | solution.py:327
  31.9 1.3 %copy.4 = f32[16,256,128]{2,1,0:T(8,128)} copy(f32[16,256,128]{2,1,0:T(8,128)S(1)} %shard_map.28) | data formatting | bytes 4194304
